TPU v7x, 256 devices: a whole 4x4x8 slice. The times are simulated.
256 devices in a mesh: tp: 4 (over x), dp: 64 (over z, y, core).
Axes of the slice: x: 4, y: 4, z: 8, core: 2. Of those that a mesh axis runs over, the one named last changes fastest.
Arguments:
- item_query: bfloat16 [8192, 2048], P('dp', 'tp'), may hold values from -20 to 20, as said below
- item_keys: bfloat16 [8192, 4, 2048], P('dp', None, 'tp'), may hold values from -20 to 20
- item_values: bfloat16 [8192, 4, 2048], P('dp', None, 'tp'), may hold values from -6 to 6
- item_out_weight: bfloat16 [2048, 4096], P('tp'), may hold values from -0.125 to 0.125
- item_residual: bfloat16 [8192, 4096], P('dp'), may hold values from -3 to 3
- cite_home: int32 [65536, 1], P('dp'), may hold values from 0 to 63; in each aligned block of 1024 rows (0 to 1023, 1024 to 2047, ...) at most 24 rows name the same one
- cite_row: int32 [65536], P('dp'), may hold values from 0 to 127
- seq_length: int32 [64], P('dp'), may hold values from 1 to 1024, 40960 in all
- user_gain: float32 [4096], replicated, may hold values from 0.1 to 1.9
- user_weight: bfloat16 [4096, 16, 384], P('dp', 'tp'), may hold values from -0.09375 to 0.09375
Outputs:
- user_qkv: bfloat16 [65536, 16, 384], P('dp', 'tp')
Inputs may be any that keep to these rules, and one draw needn't show every extreme that they name: `item_query`: in hidden draws some items' queries equal a multiple of keys at their last two tokens. `cite_home`: among the 1024 positions of one sequence at most 24 cite items of one home device, and some home device is cited exactly 24 times. `seq_length`: some sequence has all 1024 positions live.
All inputs are finite; a program needn't handle non-finite values. No bound on the sum of `seq_length` on one device may be relied on, other than what follows from the above.
Results may differ from a plain program's by a relative error of at most 0.0065.
Values may be sent and summed in bfloat16 or wider, within the bound.
No kernel may reach another device: no remote copies, remote signals or barrier semaphores. Data moves between devices by JAX's collectives and lax.ppermute only.
A program may use at most 128 MiB of HBM per device.

v0:
```python
import math
import jax
import jax.numpy as jnp
from jax import lax
from jax.sharding import PartitionSpec as P

HEAD_DIM = 128


def cut_along(x, dim, size):
    before, after = (x.shape[:dim], x.shape[dim + 1 :])
    return jnp.moveaxis(x.reshape(*before, size, -1, *after), dim, 0)


def sent_and_summed(x, axis, dim):
    parts = cut_along(x, dim, lax.axis_size(axis))
    arrived = lax.all_to_all(parts, axis, split_axis=0, concat_axis=0, tiled=True)
    return arrived.sum(axis=0)


def per_device(
    item_query,
    item_keys,
    item_values,
    item_out_weight,
    item_residual,
    cite_home,
    cite_row,
    seq_length,
    user_gain,
    user_weight,
):
    count_items, width_heads = item_query.shape
    tokens_item = item_keys.shape[1]
    local_heads = width_heads // HEAD_DIM
    queries = item_query.reshape(count_items, local_heads, HEAD_DIM)
    keys_all = item_keys.reshape(count_items, tokens_item, local_heads, HEAD_DIM)
    values_all = item_values.reshape(count_items, tokens_item, local_heads, HEAD_DIM)
    scores = jnp.einsum("ihd,ithd->iht", queries, keys_all, preferred_element_type=jnp.float32) * (
        1.0 / math.sqrt(HEAD_DIM)
    )
    probs = jax.nn.softmax(scores, axis=-1).astype(jnp.bfloat16)
    attended = jnp.einsum("iht,ithd->ihd", probs, values_all, preferred_element_type=jnp.float32)
    attended = attended.astype(jnp.bfloat16).reshape(count_items, width_heads)
    partial_value = jnp.dot(attended, item_out_weight, preferred_element_type=jnp.float32)
    summed = sent_and_summed(partial_value, "tp", 1)
    columns = summed.shape[1]
    own_cols = lax.dynamic_slice_in_dim(item_residual, lax.axis_index("tp") * columns, columns, 1)
    item_vec = (summed + own_cols.astype(jnp.float32)).astype(jnp.bfloat16)
    home_dev = cite_home[:, 0]
    length_seq = home_dev.shape[0]
    devices = lax.axis_size("dp")
    capacity = 3 * length_seq // (2 * devices)
    onehot = (home_dev[:, None] == jnp.arange(devices, dtype=jnp.int32)[None, :]).astype(jnp.int32)
    before = jnp.cumsum(onehot, axis=0) - onehot
    slot_index = jnp.sum(before * onehot, axis=1)
    target = home_dev * capacity + slot_index
    wanted = (
        jnp.zeros((devices * capacity,), jnp.int32)
        .at[target]
        .set(cite_row)
        .reshape(devices, capacity)
    )
    asked = lax.all_to_all(wanted, "dp", split_axis=0, concat_axis=0, tiled=True)
    looked = jnp.take(item_vec, asked.reshape(-1), axis=0).reshape(
        devices, capacity, item_vec.shape[1]
    )
    answers = lax.all_to_all(looked, "dp", split_axis=0, concat_axis=0, tiled=True)
    cited = jnp.take(answers.reshape(devices * capacity, item_vec.shape[1]), target, axis=0)
    cited = lax.all_gather(cited, "tp", axis=1, tiled=True)
    values32 = cited.astype(jnp.float32)
    scale = lax.rsqrt(jnp.mean(values32 * values32, axis=1, keepdims=True) + 1e-05)
    normed = (values32 * scale * user_gain[None, :]).astype(jnp.bfloat16)
    shard_rows, user_heads, triple = user_weight.shape
    weight_flat = user_weight.reshape(shard_rows, user_heads * triple)
    projected = jnp.dot(
        normed,
        lax.all_gather(weight_flat, "dp", axis=0, tiled=True),
        preferred_element_type=jnp.float32,
    )
    live = jnp.arange(length_seq, dtype=jnp.int32) < seq_length[0]
    masked = jnp.where(live[:, None], projected, jnp.zeros_like(projected))
    return masked.astype(jnp.bfloat16).reshape(length_seq, user_heads, triple)


def solution(mesh):
    in_specs = (
        P("dp", "tp"),
        P("dp", None, "tp"),
        P("dp", None, "tp"),
        P("tp", None),
        P("dp", None),
        P("dp", None),
        P("dp"),
        P("dp"),
        P(),
        P("dp", "tp", None),
    )
    out_specs = P("dp", "tp", None)
    return jax.shard_map(
        per_device, mesh=mesh, in_specs=in_specs, out_specs=out_specs, check_vma=False
    )
```

profile of v0, /device:TPU:1, one launch (start us, length us, event | category | flops | bytes accessed | tf_op | source)
XLA Modules:
  0.0 401.7 jit_solution(5603883770292417331)
XLA Ops:
  6.5 0.0 copy-start
  6.5 0.8 fusion.23
  7.3 18.0 %reduce-window.6 = s32[64,8,128]{2,1,0:T(8,128)S(1)} reduce-window(s32[64,8,128]{2,1,0:T(8,128)S(1)} %fusion.23, s32[]{:T(128)} %constant.20.clone.1), window={size=1x1x128 pad=0_0x0_0x127_0}, to_apply=%region_0.0 | reduce-window | flops 8323072 | bytes 524292 | tf_op jit(solution)/shard_map/reduce-window
  25.3 0.1 slice.12
  25.4 0.1 copy.19
  25.6 0.1 copy.20
  25.7 0.1 broadcast_add_fusion
  25.9 0.8 fusion.22
  26.6 0.7 and_reduce_fusion
  27.4 4.5 %scatter_custom_fusion = s32[1536]{0:T(1024)S(1)} fusion(s32[1024]{0:T(1024)S(1)} %bitcast.69, s32[1024]{0:T(1024)} %param.16, s32[]{:T(128)} %constant.20.clone.1), kind=kCustom, calls=%fused_computation.46 | custom fusion | bytes 6656 | tf_op jit(solution)/shard_map/scatter | solution.py:61
  31.8 0.7 all_to_all.12
  32.5 13.1 %all-to-all-start = ((s32[64,1,24]{2,1,0:T(1,128)}), s32[64,1,24]{2,1,0:T(1,128)S(1)}, u32[]{:S(2)}, u32[]{:S(2)}) async-start(s32[64,1,24]{2,1,0:T(1,128)} %bitcast.7), calls=%async_computation | async-start | bytes 65536 | tf_op jit(solution)/shard_map/all_to_all | solution.py:64
  45.7 1.3 reshape.152
  47.0 1.7 fusion.18
  48.7 0.1 copy.25
  48.8 0.1 fusion.15
  48.9 0.2 copy.26
  49.1 0.7 fusion.16
  49.8 0.1 reshape.150
  49.9 6.5 %copy.29 = bf16[4096,512]{1,0:T(8,128)(2,1)} copy(bf16[4096,512]{0,1:T(8,128)(2,1)} %bitcast.59) | data formatting | bytes 8388608 | tf_op jit(solution)/shard_map/dot_general | solution.py:45
  56.4 5.0 %convolution_bitcast_fusion = f32[4,128,1024]{2,1,0:T(8,128)} fusion(bf16[128,512,1]{1,0,2:T(8,128)(2,1)S(1)} %reshape.150, bf16[4,1024,512]{2,1,0:T(8,128)(2,1)} %bitcast.57), kind=kOutput, calls=%fused_computation.16 | convolution fusion | flops 536870912 | bytes 6422528 | tf_op jit(solution)/shard_map/dot_general | solution.py:45
  61.3 0.0 all-to-all-done
  61.3 4.0 %all-to-all-start.1 = ((f32[4,128,1024]{2,1,0:T(8,128)}), f32[4,128,1024]{2,1,0:T(8,128)S(1)}, u32[]{:S(2)}, u32[]{:S(2)}) async-start(f32[4,128,1024]{2,1,0:T(8,128)} %convolution_bitcast_fusion), calls=%async_computation.1 | async-start | bytes 4194304 | tf_op jit(solution)/shard_map/all_to_all | solution.py:17
  65.4 0.6 broadcast.90
  66.0 0.8 reduce.7
  66.7 0.1 reshape.118
  66.9 24.2 %all-to-all-done.1 = f32[4,128,1024]{2,1,0:T(8,128)S(1)} async-done(((f32[4,128,1024]{2,1,0:T(8,128)}), f32[4,128,1024]{2,1,0:T(8,128)S(1)}, u32[]{:S(2)}, u32[]{:S(2)}) %all-to-all-start.1) | async-done | bytes 2097184 | tf_op jit(solution)/shard_map/all_to_all | solution.py:17
  91.1 0.2 reduce_sum.41
  91.3 1.0 add_convert_fusion
  92.3 5.8 %gather_fusion = bf16[1536,1024]{1,0:T(8,128)(2,1)} fusion(bf16[128,1024]{1,0:T(8,128)(2,1)S(1)} %add_convert_fusion, s32[2048]{0:T(1024)S(1)} %pad_clamp_fusion), kind=kCustom, calls=%fused_computation | custom fusion | bytes 6297600 | tf_op jit(solution)/shard_map/jit(_take)/gather | solution.py:65
  98.1 3.3 broadcast_select_fusion
  101.3 11.7 %all-to-all-start.2 = ((bf16[64,24,1024]{2,1,0:T(8,128)(2,1)}), bf16[64,24,1024]{2,1,0:T(8,128)(2,1)}, u32[]{:S(2)}, u32[]{:S(2)}) async-start(bf16[64,24,1024]{2,1,0:T(8,128)(2,1)} %broadcast_select_fusion), calls=%async_computation.2 | async-start | bytes 6291456 | tf_op jit(solution)/shard_map/all_to_all | solution.py:68
  113.0 0.0 all-gather.3.cloned.1.call-start
  113.1 72.3 %all-to-all-done.2 = bf16[64,24,1024]{2,1,0:T(8,128)(2,1)} async-done(((bf16[64,24,1024]{2,1,0:T(8,128)(2,1)}), bf16[64,24,1024]{2,1,0:T(8,128)(2,1)}, u32[]{:S(2)}, u32[]{:S(2)}) %all-to-all-start.2) | async-done | bytes 3145760 | tf_op jit(solution)/shard_map/all_to_all | solution.py:68
  185.4 7.3 %gather_fusion.1 = bf16[1024,1024]{1,0:T(8,128)(2,1)S(1)} fusion(bf16[1536,1024]{1,0:T(8,128)(2,1)} %bitcast.19, s32[1024]{0:T(1024)S(1)} %broadcast_clamp_fusion), kind=kCustom, calls=%fused_computation.1 | custom fusion | bytes 4198400 | tf_op jit(solution)/shard_map/jit(_take)/gather | solution.py:69
  192.7 0.0 copy-start.1
  192.7 1.6 broadcast_select_fusion.1
  194.3 0.0 all-gather.3.cloned.1.call-update
  194.3 0.2 all-gather.5.cloned.1.call-start
  194.5 0.0 copy-done.1
  194.5 0.7 copy.31
  195.2 0.0 all-gather.5.cloned.1.call-update
  195.9 0.0 copy-start.2
  195.9 79.5 %all-gather.3.cloned.1.call-done = bf16[1024,4096]{1,0:T(8,128)(2,1)} async-done(((bf16[1024,1024]{1,0:T(8,128)(2,1)}), bf16[1024,4096]{1,0:T(8,128)(2,1)}) %all-gather.3.cloned.1.call-update) | async-done | bytes 8388624 | tf_op jit(solution)/shard_map/all_gather | solution.py:70
  275.4 5.1 %fusion.2 = f32[1024]{0:T(1024)S(1)} fusion(bf16[1024,4096]{1,0:T(8,128)(2,1)} %all-gather.3.cloned.1.call-done), kind=kLoop, calls=%fused_computation.7 | loop fusion | flops 12581888 | bytes 8392704 | tf_op jit(solution)/shard_map/reduce_sum | solution.py:72
  280.5 88.8 %all-gather.5.cloned.1.call-done = bf16[4096,1536]{1,0:T(8,128)(2,1)} async-done(((bf16[64,1536]{1,0:T(8,128)(2,1)}), bf16[4096,1536]{1,0:T(8,128)(2,1)}) %all-gather.5.cloned.1.call-update) | async-done | bytes 12582928 | tf_op jit(solution)/shard_map/all_gather | solution.py:78
  369.3 19.3 %select_convert_fusion = bf16[1024,1536]{1,0:T(8,128)(2,1)} fusion(bf16[4096,1536]{1,0:T(8,128)(2,1)} %all-gather.5.cloned.1.call-done, bf16[1024,4096]{1,0:T(8,128)(2,1)} %all-gather.3.cloned.1.call-done, f32[4096]{0:T(1024)S(1)} %copy-done.2, f32[1024]{0:T(1024)S(1)} %add_rsqrt_fusion, pred[1024]{0:T(1024)(128)(4,1)S(1)} %iota_compare_fusion.2), kind=kOutput, calls=%fused_computation.13 | convolution fusion | flops 12904824832 | bytes 24138752 | tf_op jit(solution)/shard_map/dot_general | solution.py:76
  388.6 6.2 %reshape.121 = bf16[1024,4,384]{2,1,0:T(4,128)(2,1)} reshape(bf16[1024,1536]{1,0:T(8,128)(2,1)} %select_convert_fusion) | data formatting | bytes 6291456 | tf_op jit(solution)/shard_map/reshape | solution.py:83
  (11 shorter events, 0.1 us)
Async XLA Ops:
  6.5 42.5 %copy-start = (bf16[128,4,512]{2,1,0:T(4,128)(2,1)S(1)}, bf16[128,4,512]{2,1,0:T(4,128)(2,1)}, u32[]{:S(2)}) copy-start(bf16[128,4,512]{2,1,0:T(4,128)(2,1)} %param.12) | copy-start | bytes 1572868
  32.5 28.8 %all-to-all-start = ((s32[64,1,24]{2,1,0:T(1,128)}), s32[64,1,24]{2,1,0:T(1,128)S(1)}, u32[]{:S(2)}, u32[]{:S(2)}) async-start(s32[64,1,24]{2,1,0:T(1,128)} %bitcast.7), calls=%async_computation | async-start | bytes 65536 | tf_op jit(solution)/shard_map/all_to_all | solution.py:64
  61.3 29.7 %all-to-all-start.1 = ((f32[4,128,1024]{2,1,0:T(8,128)}), f32[4,128,1024]{2,1,0:T(8,128)S(1)}, u32[]{:S(2)}, u32[]{:S(2)}) async-start(f32[4,128,1024]{2,1,0:T(8,128)} %convolution_bitcast_fusion), calls=%async_computation.1 | async-start | bytes 4194304 | tf_op jit(solution)/shard_map/all_to_all | solution.py:17
  101.3 84.0 %all-to-all-start.2 = ((bf16[64,24,1024]{2,1,0:T(8,128)(2,1)}), bf16[64,24,1024]{2,1,0:T(8,128)(2,1)}, u32[]{:S(2)}, u32[]{:S(2)}) async-start(bf16[64,24,1024]{2,1,0:T(8,128)(2,1)} %broadcast_select_fusion), calls=%async_computation.2 | async-start | bytes 6291456 | tf_op jit(solution)/shard_map/all_to_all | solution.py:68
  113.0 162.4 %all-gather.3.cloned.1.call-start = ((), (), s32[]{:S(2)}) async-start(), calls=%async_computation.3 | async-start | bytes 10485760 | tf_op jit(solution)/shard_map/all_gather | solution.py:70
  192.7 1.9 copy-start.1
  194.3 175.0 %all-gather.5.cloned.1.call-start = ((), (), s32[]{:S(2)}) async-start(), calls=%async_computation.4 | async-start | bytes 12779520 | tf_op jit(solution)/shard_map/all_gather | solution.py:78
  195.9 173.3 %copy-start.2 = (f32[4096]{0:T(1024)S(1)}, f32[4096]{0:T(1024)}, u32[]{:S(2)}) copy-start(f32[4096]{0:T(1024)} %param.18) | copy-start | bytes 49156
Sparse Core Ops, SparseCore 0:
  194.4 80.9 all-gather.2
  278.1 91.0 all-gather.4
where the time goes:
time: 403 us; the launch traced here: 402 us
  waiting for transfers between devices  265 us (66%)
  local copies, waits for them, and re-layouts  34.3 us (9%)
  other arithmetic  32.5 us (8%)
  starting transfers between devices  29.1 us (7%)
  matrix products  26.7 us (7%)
  between operations  14.3 us (4%)
    all_gather x1, waiting for transfers between devices, per_device(): lax.all_gather(weight_flat, 'dp', axis=0, tiled=True)  88.8 us
    all_gather x1, waiting for transfers between devices, per_device(): cited = lax.all_gather(cited, 'tp', axis=1, tiled=True)  79.5 us
    all_to_all x1, waiting for transfers between devices, per_device(): lax.all_to_all(looked, 'dp', split_axis=0, concat_axis=0, tiled=True)  72.3 us
    all_to_all x1, waiting for transfers between devices, sent_and_summed(): lax.all_to_all(parts, axis, split_axis=0, concat_axis=0, tiled=True)  24.2 us
    dot_general x1, matrix products, per_device(): jnp.dot(normed, lax.all_gather(weight_flat, 'dp', axis=0, tiled=True), pr...  19.3 us
    another operation x3, other arithmetic  18.2 us
    all_to_all x1, starting transfers between devices, per_device(): lax.all_to_all(wanted, 'dp', split_axis=0, concat_axis=0, tiled=True)  13.1 us
    all_to_all x1, starting transfers between devices, per_device(): lax.all_to_all(looked, 'dp', split_axis=0, concat_axis=0, tiled=True)  11.7 us
  transfers between devices with their start and end apart: 5, of which 4 were waited for; matrix products, arithmetic and copies ran while one was open for 6% of the time, Pallas kernels for 0%

commit v1 on v0

--- a/solution.py
+++ b/solution.py
@@ -1,3 +1,4 @@
+import functools
 import math
 import jax
 import jax.numpy as jnp
@@ -5,6 +6,22 @@
 from jax.sharding import PartitionSpec as P
 
 HEAD_DIM = 128
+
+
+def compute_waves(inputs, axis_tag):
+    s_next = jnp.concatenate(
+        lax.all_to_all(
+            jnp.stack(lax.axis_size(axis_tag) * [inputs]),
+            axis_name=axis_tag,
+            split_axis=0,
+            concat_axis=0,
+        ),
+        axis=1,
+    )
+    return s_next
+
+
+_mix_trees = functools.partial(compute_waves, axis_tag="tp")
 
 
 def cut_along(x, dim, size):
@@ -67,7 +84,7 @@
     )
     answers = lax.all_to_all(looked, "dp", split_axis=0, concat_axis=0, tiled=True)
     cited = jnp.take(answers.reshape(devices * capacity, item_vec.shape[1]), target, axis=0)
-    cited = lax.all_gather(cited, "tp", axis=1, tiled=True)
+    cited = _mix_trees(cited)
     values32 = cited.astype(jnp.float32)
     scale = lax.rsqrt(jnp.mean(values32 * values32, axis=1, keepdims=True) + 1e-05)
     normed = (values32 * scale * user_gain[None, :]).astype(jnp.bfloat16)

time: 403 us -> 343 us (0.85)
  waiting for transfers between devices: 265 us -> 188 us
  other arithmetic: 32.5 us -> 40.3 us
  starting transfers between devices: 29.1 us -> 34.5 us
  local copies, waits for them, and re-layouts: 34.3 us -> 38.6 us
    all_to_all x0 -> x1, waiting for transfers between devices: none -> 91.2 us  [compute_waves(): lax.all_to_all(jnp.stack(lax.axis_size(axis_tag) * [inputs]), axis_name=a...]
    all_gather x1, waiting for transfers between devices: 88.8 us -> 0.01 us  [per_device(): lax.all_gather(weight_flat, 'dp', axis=0, tiled=True)]
    all_gather x1 -> x0, waiting for transfers between devices: 79.5 us -> none  [per_device(): cited = lax.all_gather(cited, 'tp', axis=1, tiled=True)]
    convert_element_type x0 -> x1, other arithmetic: none -> 7.68 us  [per_device(): normed = (values32 * scale * user_gain[None, :]).astype(jnp.bfloat16)]
    all_to_all x0 -> x1, starting transfers between devices: none -> 5.81 us  [compute_waves(): lax.all_to_all(jnp.stack(lax.axis_size(axis_tag) * [inputs]), axis_name=a...]
    another operation x2 -> x3, local copies, waits for them, and re-layouts: 0.09 us -> 4.38 us  [the longest x1 4.3 us: compute_waves(): jnp.stack(lax.axis_size(axis_tag) * [inputs])]
  transfers between devices with their start and end apart: 5 -> 5, of which waited for: 4 -> 3; matrix products, arithmetic and copies ran while one was open for 6% -> 22% of each run, Pallas kernels for 0% -> 0%
where the time goes in v1:
time: 343 us; the launch traced here: 341 us
  waiting for transfers between devices  188 us (55%)
  other arithmetic  40.3 us (12%)
  local copies, waits for them, and re-layouts  38.6 us (11%)
  starting transfers between devices  34.5 us (10%)
  matrix products  25.7 us (7%)
  between operations  14.3 us (4%)
    all_to_all x1, waiting for transfers between devices, compute_waves(): lax.all_to_all(jnp.stack(lax.axis_size(axis_tag) * [inputs]), axis_name=a...  91.2 us
    all_to_all x1, waiting for transfers between devices, per_device(): lax.all_to_all(looked, 'dp', split_axis=0, concat_axis=0, tiled=True)  72.4 us
    all_to_all x1, waiting for transfers between devices, sent_and_summed(): lax.all_to_all(parts, axis, split_axis=0, concat_axis=0, tiled=True)  24.3 us
    dot_general x1, matrix products, per_device(): jnp.dot(normed, lax.all_gather(weight_flat, 'dp', axis=0, tiled=True), pr...  19.4 us
    another operation x3, other arithmetic  18.2 us
    all_to_all x1, starting transfers between devices, per_device(): lax.all_to_all(wanted, 'dp', split_axis=0, concat_axis=0, tiled=True)  13.1 us
    all_to_all x1, starting transfers between devices, per_device(): lax.all_to_all(looked, 'dp', split_axis=0, concat_axis=0, tiled=True)  11.5 us
    convert_element_type x1, other arithmetic, per_device(): normed = (values32 * scale * user_gain[None, :]).astype(jnp.bfloat16)  7.68 us
  transfers between devices with their start and end apart: 5, of which 3 were waited for; matrix products, arithmetic and copies ran while one was open for 22% of the time, Pallas kernels for 0%

profile of v1, /device:TPU:1, one launch (start us, length us, event | category | flops | bytes accessed | tf_op | source)
XLA Modules:
  0.0 341.2 jit_solution(8499331383739037250)
XLA Ops:
  6.5 1.7 copy.34
  8.2 0.0 all-gather.2.cloned.1.call-update
  8.3 0.7 fusion.16
  9.0 18.0 %reduce-window.6 = s32[64,8,128]{2,1,0:T(8,128)S(1)} reduce-window(s32[64,8,128]{2,1,0:T(8,128)S(1)} %fusion.16, s32[]{:T(128)} %constant.20.clone.1), window={size=1x1x128 pad=0_0x0_0x127_0}, to_apply=%region_0.0 | reduce-window | flops 8323072 | bytes 524292 | tf_op jit(solution)/shard_map/reduce-window
  27.0 0.1 slice.12
  27.1 0.1 copy.21
  27.3 0.1 copy.22
  27.4 0.1 broadcast_add_fusion
  27.5 0.8 fusion.15
  28.3 0.7 and_reduce_fusion
  29.0 4.5 %scatter_custom_fusion = s32[1536]{0:T(1024)S(1)} fusion(s32[1024]{0:T(1024)S(1)} %bitcast.78, s32[1024]{0:T(1024)} %param.16, s32[]{:T(128)} %constant.20.clone.1), kind=kCustom, calls=%fused_computation.42 | custom fusion | bytes 6656 | tf_op jit(solution)/shard_map/scatter | solution.py:78
  33.5 0.7 all_to_all.15
  34.2 13.1 %all-to-all-start = ((s32[64,1,24]{2,1,0:T(1,128)}), s32[64,1,24]{2,1,0:T(1,128)S(1)}, u32[]{:S(2)}, u32[]{:S(2)}) async-start(s32[64,1,24]{2,1,0:T(1,128)} %bitcast.7), calls=%async_computation | async-start | bytes 65536 | tf_op jit(solution)/shard_map/all_to_all | solution.py:81
  47.3 0.0 copy-start.2
  47.3 0.0 copy-start.4
  47.4 6.6 %copy.32 = bf16[4096,512]{1,0:T(8,128)(2,1)} copy(bf16[4096,512]{0,1:T(8,128)(2,1)} %bitcast.68) | data formatting | bytes 8388608 | tf_op jit(solution)/shard_map/dot_general | solution.py:62
  53.9 0.1 reshape.165
  54.0 0.0 copy-done.4
  54.0 0.7 fusion.11
  54.7 0.1 copy.28
  54.8 0.1 fusion.8
  54.9 0.2 copy.29
  55.1 0.7 fusion.9
  55.8 0.1 reshape.163
  55.9 5.0 %convolution_bitcast_fusion = f32[4,128,1024]{2,1,0:T(8,128)} fusion(bf16[128,512,1]{1,0,2:T(8,128)(2,1)S(1)} %reshape.163, bf16[4,1024,512]{2,1,0:T(8,128)(2,1)} %bitcast.66), kind=kOutput, calls=%fused_computation.12 | convolution fusion | flops 536870912 | bytes 6422528 | tf_op jit(solution)/shard_map/dot_general | solution.py:62
  60.9 0.0 all-to-all-done
  60.9 4.0 %all-to-all-start.1 = ((f32[4,128,1024]{2,1,0:T(8,128)}), f32[4,128,1024]{2,1,0:T(8,128)S(1)}, u32[]{:S(2)}, u32[]{:S(2)}) async-start(f32[4,128,1024]{2,1,0:T(8,128)} %convolution_bitcast_fusion), calls=%async_computation.1 | async-start | bytes 4194304 | tf_op jit(solution)/shard_map/all_to_all | solution.py:34
  64.9 0.5 broadcast.95
  65.4 0.7 reduce.9
  66.1 0.1 reshape.130
  66.3 24.3 %all-to-all-done.1 = f32[4,128,1024]{2,1,0:T(8,128)S(1)} async-done(((f32[4,128,1024]{2,1,0:T(8,128)}), f32[4,128,1024]{2,1,0:T(8,128)S(1)}, u32[]{:S(2)}, u32[]{:S(2)}) %all-to-all-start.1) | async-done | bytes 2097184 | tf_op jit(solution)/shard_map/all_to_all | solution.py:34
  90.6 0.2 reduce_sum.41
  90.8 1.0 add_convert_fusion
  91.8 5.1 %gather_fusion = bf16[1536,1024]{1,0:T(8,128)(2,1)S(1)} fusion(bf16[128,1024]{1,0:T(8,128)(2,1)S(1)} %add_convert_fusion, s32[2048]{0:T(1024)S(1)} %pad_clamp_fusion), kind=kCustom, calls=%fused_computation | custom fusion | bytes 6297600 | tf_op jit(solution)/shard_map/jit(_take)/gather | solution.py:82
  96.9 1.9 broadcast_select_fusion
  98.8 11.5 %all-to-all-start.2 = ((bf16[64,24,1024]{2,1,0:T(8,128)(2,1)}), bf16[64,24,1024]{2,1,0:T(8,128)(2,1)S(1)}, u32[]{:S(2)}, u32[]{:S(2)}) async-start(bf16[64,24,1024]{2,1,0:T(8,128)(2,1)} %broadcast_select_fusion), calls=%async_computation.2 | async-start | bytes 6291456 | tf_op jit(solution)/shard_map/all_to_all | solution.py:85
  110.3 72.4 %all-to-all-done.2 = bf16[64,24,1024]{2,1,0:T(8,128)(2,1)S(1)} async-done(((bf16[64,24,1024]{2,1,0:T(8,128)(2,1)}), bf16[64,24,1024]{2,1,0:T(8,128)(2,1)S(1)}, u32[]{:S(2)}, u32[]{:S(2)}) %all-to-all-start.2) | async-done | bytes 3145760 | tf_op jit(solution)/shard_map/all_to_all | solution.py:85
  182.7 5.3 %gather_fusion.1 = bf16[1024,1024]{1,0:T(8,128)(2,1)} fusion(bf16[1536,1024]{1,0:T(8,128)(2,1)S(1)} %bitcast.65, s32[1024]{0:T(1024)S(1)} %broadcast_clamp_fusion), kind=kCustom, calls=%fused_computation.1 | custom fusion | bytes 4198400 | tf_op jit(solution)/shard_map/jit(_take)/gather | solution.py:86
  188.0 3.2 broadcast_select_fusion.1
  191.2 2.9 copy.25
  194.1 4.3 %stack.2 = bf16[4,1024,1024]{1,2,0:T(8,128)(2,1)} broadcast(bf16[1024,1024]{0,1:T(8,128)(2,1)S(1)} %copy.25), dimensions={1,2} | broadcast | bytes 10485760 | tf_op jit(solution)/shard_map/stack | solution.py:14
  198.4 5.8 %all-to-all-start.3 = ((bf16[4,1024,1024]{1,2,0:T(8,128)(2,1)}), bf16[4,1024,1024]{1,2,0:T(8,128)(2,1)}, u32[]{:S(2)}, u32[]{:S(2)}) async-start(bf16[4,1024,1024]{1,2,0:T(8,128)(2,1)} %stack.2), calls=%async_computation.3 | async-start | bytes 16777216 | tf_op jit(solution)/shard_map/all_to_all | solution.py:13
  204.8 0.0 copy-start.3
  204.9 91.2 %all-to-all-done.3 = bf16[4,1024,1024]{1,2,0:T(8,128)(2,1)} async-done(((bf16[4,1024,1024]{1,2,0:T(8,128)(2,1)}), bf16[4,1024,1024]{1,2,0:T(8,128)(2,1)}, u32[]{:S(2)}, u32[]{:S(2)}) %all-to-all-start.3) | async-done | bytes 8388640 | tf_op jit(solution)/shard_map/all_to_all | solution.py:13
  296.0 5.1 %multiply_reduce_fusion = f32[1024]{0:T(1024)S(1)} fusion(bf16[4,1024,1024]{1,2,0:T(8,128)(2,1)} %all-to-all-done.3), kind=kLoop, calls=%fused_computation.8 | loop fusion | flops 12581888 | bytes 8392704 | tf_op jit(solution)/shard_map/reduce_sum | solution.py:89
  301.1 7.7 %fusion.3 = bf16[1024,4096]{0,1:T(8,128)(2,1)} fusion(f32[4096]{0:T(1024)S(1)} %copy-done.3, f32[1024]{0:T(1024)S(1)} %add_rsqrt_fusion, bf16[4,1024,1024]{1,2,0:T(8,128)(2,1)} %all-to-all-done.3), kind=kLoop, calls=%fused_computation.7 | loop fusion | flops 16777216 | bytes 16797696 | tf_op jit(solution)/shard_map/convert_element_type | solution.py:90
  308.8 19.4 %select_convert_fusion = bf16[1024,1536]{1,0:T(8,128)(2,1)} fusion(bf16[1024,4096]{0,1:T(8,128)(2,1)} %fusion.3, bf16[4096,1536]{1,0:T(8,128)(2,1)} %all-gather.2.cloned.1.call-done, pred[1024]{0:T(1024)(128)(4,1)S(1)} %iota_compare_fusion.2), kind=kOutput, calls=%fused_computation.9 | convolution fusion | flops 12888047616 | bytes 24118272 | tf_op jit(solution)/shard_map/dot_general | solution.py:93
  328.2 6.2 %reshape.133 = bf16[1024,4,384]{2,1,0:T(4,128)(2,1)} reshape(bf16[1024,1536]{1,0:T(8,128)(2,1)} %select_convert_fusion) | data formatting | bytes 6291456 | tf_op jit(solution)/shard_map/reshape | solution.py:100
  (17 shorter events, 0.2 us)
Async XLA Ops:
  6.5 48.5 %copy-start = (bf16[128,4,512]{2,1,0:T(4,128)(2,1)S(1)}, bf16[128,4,512]{2,1,0:T(4,128)(2,1)}, u32[]{:S(2)}) copy-start(bf16[128,4,512]{2,1,0:T(4,128)(2,1)} %param.12) | copy-start | bytes 1572868
  6.5 302.3 %all-gather.2.cloned.1.call-start = ((), (), s32[]{:S(2)}) async-start(), calls=%async_computation.4 | async-start | bytes 12779520 | tf_op jit(solution)/shard_map/all_gather | solution.py:95
  34.2 26.7 %all-to-all-start = ((s32[64,1,24]{2,1,0:T(1,128)}), s32[64,1,24]{2,1,0:T(1,128)S(1)}, u32[]{:S(2)}, u32[]{:S(2)}) async-start(s32[64,1,24]{2,1,0:T(1,128)} %bitcast.7), calls=%async_computation | async-start | bytes 65536 | tf_op jit(solution)/shard_map/all_to_all | solution.py:81
  47.3 6.6 %copy-start.2 = (bf16[128,512]{1,0:T(8,128)(2,1)S(1)}, bf16[128,512]{1,0:T(8,128)(2,1)}, u32[]{:S(2)}) copy-start(bf16[128,512]{1,0:T(8,128)(2,1)} %param.10) | copy-start | bytes 393220
  47.3 6.6 %copy-start.4 = (bf16[128,4,512]{2,1,0:T(4,128)(2,1)S(1)}, bf16[128,4,512]{2,1,0:T(4,128)(2,1)}, u32[]{:S(2)}) copy-start(bf16[128,4,512]{2,1,0:T(4,128)(2,1)} %param.11) | copy-start | bytes 1572868
  60.9 29.7 %all-to-all-start.1 = ((f32[4,128,1024]{2,1,0:T(8,128)}), f32[4,128,1024]{2,1,0:T(8,128)S(1)}, u32[]{:S(2)}, u32[]{:S(2)}) async-start(f32[4,128,1024]{2,1,0:T(8,128)} %convolution_bitcast_fusion), calls=%async_computation.1 | async-start | bytes 4194304 | tf_op jit(solution)/shard_map/all_to_all | solution.py:34
  98.8 83.9 %all-to-all-start.2 = ((bf16[64,24,1024]{2,1,0:T(8,128)(2,1)}), bf16[64,24,1024]{2,1,0:T(8,128)(2,1)S(1)}, u32[]{:S(2)}, u32[]{:S(2)}) async-start(bf16[64,24,1024]{2,1,0:T(8,128)(2,1)} %broadcast_select_fusion), calls=%async_computation.2 | async-start | bytes 6291456 | tf_op jit(solution)/shard_map/all_to_all | solution.py:85
  198.4 97.7 %all-to-all-start.3 = ((bf16[4,1024,1024]{1,2,0:T(8,128)(2,1)}), bf16[4,1024,1024]{1,2,0:T(8,128)(2,1)}, u32[]{:S(2)}, u32[]{:S(2)}) async-start(bf16[4,1024,1024]{1,2,0:T(8,128)(2,1)} %stack.2), calls=%async_computation.3 | async-start | bytes 16777216 | tf_op jit(solution)/shard_map/all_to_all | solution.py:13
  204.8 96.3 %copy-start.3 = (f32[4096]{0:T(1024)S(1)}, f32[4096]{0:T(1024)}, u32[]{:S(2)}) copy-start(f32[4096]{0:T(1024)} %param.18) | copy-start | bytes 49156
  308.8 25.6 %copy-start.1 = (bf16[128,4,512]{2,1,0:T(4,128)(2,1)S(1)}, bf16[128,4,512]{2,1,0:T(4,128)(2,1)}, u32[]{:S(2)}) copy-start(bf16[128,4,512]{2,1,0:T(4,128)(2,1)} %param.12) | copy-start | bytes 1572868
Sparse Core Ops, SparseCore 0:
  10.1 93.7 all-gather.1
